TPU v7x, 32 devices: a whole 2x2x4 slice. The times are simulated.
32 devices in a mesh: cell: 16 (over z, y, x), gene: 2 (over core).
Axes of the slice: x: 2, y: 2, z: 4, core: 2. Of those that a mesh axis runs over, the one named last changes fastest.
Arguments:
- tiles: bfloat16 [2, 1024, 128, 128], P('gene', 'cell'), may hold values from -8 to 8
- tile_row: int32 [2, 1024], P('gene', 'cell'), may hold values from 0 to 7, as said below
- tile_col: int32 [2, 1024], P('gene', 'cell'), may hold values from 0 to 15
- tile_count: int32 [2, 16], P('gene', 'cell'), may hold values from 1 to 64, as said below
- start_basis: bfloat16 [64, 4096], P(None, 'gene'), may hold values from -0.09375 to 0.09375
Outputs:
- basis: bfloat16 [64, 16384], P(None, 'cell')
- loadings: float32 [64, 4096], P(None, ('gene', 'cell'))
Inputs may be any that keep to these rules, and one draw needn't show every extreme that they name: `tile_row`: tile row of each slot, within 0 to 7; the slots of one device name distinct (row, column) pairs. `tile_count`: slots in use; for each index of gene some device uses all 64.
All inputs are finite; a program needn't handle non-finite values.
Results may differ from a plain program's by a relative error of at most 0.018.
Values may be sent and summed in bfloat16 or wider, within the bound.
No kernel may reach another device: no remote copies, remote signals or barrier semaphores. Data moves between devices by JAX's collectives and lax.ppermute only.
A program may use at most 64 MiB of HBM per device.

v0:
```python
import jax
import jax.numpy as jnp
from jax import lax
from jax.sharding import PartitionSpec as P

ROW_BLOCKS = 8


def solve_lower(lower, right):
    return lax.linalg.triangular_solve(lower, right, left_side=True, lower=True)


def gram_of(scores):
    return jnp.dot(
        scores, scores.T, precision=lax.Precision.HIGHEST, preferred_element_type=jnp.float32
    )


def orthonormal(scores, first_total):
    first = first_total(gram_of(scores))
    lower_one = jnp.linalg.cholesky(first)
    return solve_lower(lower_one, scores)


def local(tiles, tile_row, tile_col, tile_count, start_basis):
    blocks_local = tiles[0]
    slot_count = blocks_local.shape[0]
    tile_size = blocks_local.shape[-1]
    width = start_basis.shape[0]
    gene_dev = start_basis.shape[1]
    gene_blocks = gene_dev // tile_size
    row_blocks = ROW_BLOCKS
    cell_dev = row_blocks * tile_size
    row_index = tile_row[0]
    col_index = tile_col[0]
    live = jnp.arange(slot_count) < tile_count[0, 0]
    row_target = jnp.where(live, row_index, row_blocks)
    col_target = jnp.where(live, col_index, gene_blocks)

    def first_total(gram):
        return lax.psum(gram, ("cell", "gene"))

    def merge_halves(partial_scores):
        return lax.psum_scatter(partial_scores, "gene", scatter_dimension=1, tiled=True)

    def scores_of(basis):
        picked = jnp.take(basis.reshape(width, gene_blocks, tile_size), col_index, axis=1)
        products = jnp.einsum(
            "ksg,srg->skr", picked, blocks_local, preferred_element_type=jnp.float32
        )
        summed = jax.ops.segment_sum(products, row_target, num_segments=row_blocks + 1)[:row_blocks]
        return merge_halves(jnp.transpose(summed, (1, 0, 2)).reshape(width, cell_dev))

    def loadings_of(ortho_half):
        picked = jnp.take(ortho_half.reshape(width, row_blocks, tile_size), row_index, axis=1)
        products = jnp.einsum(
            "ksr,srg->skg", picked, blocks_local, preferred_element_type=jnp.float32
        )
        summed = jax.ops.segment_sum(products, col_target, num_segments=gene_blocks + 1)[
            :gene_blocks
        ]
        return jnp.transpose(summed, (1, 0, 2)).reshape(width, gene_dev)

    ortho = orthonormal(scores_of(start_basis), first_total)
    ortho_half = ortho.astype(jnp.bfloat16)
    ortho_rows = lax.all_gather(ortho_half, "gene", axis=1, tiled=True)
    partial_value = loadings_of(ortho_rows)
    next_basis = lax.psum(partial_value, "cell").astype(jnp.bfloat16)
    ortho_two = orthonormal(scores_of(next_basis), first_total)
    scale = jnp.sqrt(jnp.float32(lax.axis_size("cell") * cell_dev))
    ortho_two_half = ortho_two.astype(jnp.bfloat16)
    basis_piece = (ortho_two * scale).astype(jnp.bfloat16)
    final_rows, basis = (
        lax.all_gather(ortho_two_half, "gene", axis=1, tiled=True),
        lax.all_gather(basis_piece, "gene", axis=1, tiled=True),
    )
    loadings = lax.psum_scatter(loadings_of(final_rows), "cell", scatter_dimension=1, tiled=True)
    return (basis, loadings)


def solution(mesh):
    return jax.shard_map(
        local,
        mesh=mesh,
        in_specs=(
            P("gene", "cell", None, None),
            P("gene", "cell"),
            P("gene", "cell"),
            P("gene", "cell"),
            P(None, "gene"),
        ),
        out_specs=(P(None, "cell"), P(None, ("gene", "cell"))),
        check_vma=False,
    )
```

profile of v0, /device:TPU:0, one launch (start us, length us, event | category | flops | bytes accessed | tf_op | source)
XLA Modules:
  0.0 349.9 jit_solution(15291023441210544630)
XLA Ops:
  7.2 0.8 compare_select_fusion
  8.7 1.0 copy_bitcast_fusion.5
  10.4 0.7 gather_fusion
  11.2 2.9 fusion.6
  14.1 7.1 %scatter_fusion = f32[9,64,128]{2,1,0:T(8,128)S(1)} fusion(f32[9,64,128]{2,1,0:T(8,128)S(1)} %broadcast.69.clone, s32[64]{0:T(128)S(1)} %get-tuple-element.8, f32[64,64,128]{2,1,0:T(8,128)} %fusion.6), kind=kCustom, calls=%fused_computation.4 | custom fusion | flops 524288 | bytes 6291712 | tf_op jit(solution)/shard_map/scatter-add | solution.py:51
  22.0 10.5 %reduce-scatter.4.cloned.1.call-done = f32[64,512]{1,0:T(8,128)} async-done(((f32[64,1024]{1,0:T(8,128)}), f32[64,512]{1,0:T(8,128)}) %reduce-scatter.4.cloned.1.call-update) | async-done | bytes 131088 | tf_op jit(solution)/shard_map/reduce_scatter | solution.py:44
  32.5 1.2 fusion.40
  33.8 40.5 %psum.21 = f32[64,64]{0,1:T(8,128)S(1)} all-reduce(f32[64,64]{0,1:T(8,128)S(1)} %fusion.40), channel_id=1, replica_groups=mesh['cell'=16,'gene'=2] {'cell','gene'}, use_global_device_ids=true, to_apply=%region_2.4 | all-reduce | flops 4096 | bytes 32768 | tf_op jit(solution)/shard_map/psum | solution.py:41
  74.4 5.8 %cholesky.44 = f32[64,64]{1,0:T(8,128)S(1)} custom-call(f32[64,64]{1,0:T(8,128)S(1)} %fusion.30), custom_call_target="Cholesky" | custom-call | tf_op jit(solution)/shard_map/jit(cholesky)/cholesky | solution.py:21
  81.6 4.9 %custom-call.6 = f32[1,64,64]{1,2,0:T(8,128)S(1)} custom-call(f32[1,64,64]{2,1,0:T(8,128)S(1)} %fusion.24), custom_call_target="InvertDiagBlocksLowerTriangular" | custom-call | tf_op jit(solution)/shard_map/triangular_solve/custom-call.0 | solution.py:10
  86.5 1.2 convolution_convert_fusion
  87.7 1.9 all_gather.9
  89.7 0.7 gather_fusion.1
  90.4 2.1 fusion.4
  92.6 7.1 %scatter_fusion.1 = f32[17,64,128]{2,1,0:T(8,128)S(1)} fusion(f32[17,64,128]{2,1,0:T(8,128)S(1)} %broadcast.70.clone, s32[64]{0:T(128)S(1)} %get-tuple-element.9, f32[64,64,128]{2,1,0:T(8,128)} %fusion.4), kind=kCustom, calls=%fused_computation.5 | custom fusion | flops 524288 | bytes 6291712 | tf_op jit(solution)/shard_map/scatter-add | solution.py:59
  99.7 81.7 %all-reduce.1 = bf16[64,2048]{1,0:T(8,128)(2,1)S(1)} all-reduce(f32[64,2048]{1,0:T(8,128)S(1)} %copy_bitcast_fusion.1), channel_id=1, replica_groups=mesh['cell'=16,'gene'=2] {'cell'}, use_global_device_ids=true, to_apply=%region_6.11 | all-reduce | flops 131072 | bytes 786432 | tf_op jit(solution)/shard_map/psum | solution.py:68
  181.4 0.8 gather_fusion.2
  182.2 2.9 fusion.2
  185.1 7.1 %scatter_fusion.2 = f32[9,64,128]{2,1,0:T(8,128)S(1)} fusion(f32[9,64,128]{2,1,0:T(8,128)S(1)} %broadcast.69, s32[64]{0:T(128)S(1)} %get-tuple-element.8, f32[64,64,128]{2,1,0:T(8,128)} %fusion.2), kind=kCustom, calls=%fused_computation.6 | custom fusion | flops 524288 | bytes 6291712 | tf_op jit(solution)/shard_map/scatter-add | solution.py:51
  192.9 4.2 %reduce-scatter.6.cloned.1.call-done = f32[64,512]{1,0:T(8,128)} async-done(((f32[64,1024]{1,0:T(8,128)}), f32[64,512]{1,0:T(8,128)}) %reduce-scatter.6.cloned.1.call-update) | async-done | bytes 131088 | tf_op jit(solution)/shard_map/reduce_scatter | solution.py:44
  197.1 1.2 fusion.41
  198.4 40.8 %psum.23 = f32[64,64]{0,1:T(8,128)S(1)} all-reduce(f32[64,64]{0,1:T(8,128)S(1)} %fusion.41), channel_id=1, replica_groups=mesh['cell'=16,'gene'=2] {'cell','gene'}, use_global_device_ids=true, to_apply=%region_9.14 | all-reduce | flops 4096 | bytes 32768 | tf_op jit(solution)/shard_map/psum | solution.py:41
  239.2 5.8 %cholesky.55 = f32[64,64]{1,0:T(8,128)S(1)} custom-call(f32[64,64]{1,0:T(8,128)S(1)} %fusion.28), custom_call_target="Cholesky" | custom-call | tf_op jit(solution)/shard_map/jit(cholesky)/cholesky | solution.py:21
  246.4 4.9 %custom-call.7 = f32[1,64,64]{1,2,0:T(8,128)S(1)} custom-call(f32[1,64,64]{2,1,0:T(8,128)S(1)} %fusion.25), custom_call_target="InvertDiagBlocksLowerTriangular" | custom-call | tf_op jit(solution)/shard_map/triangular_solve/custom-call.0 | solution.py:10
  251.3 1.2 fusion.39
  252.6 1.9 all_gather.11
  254.5 0.7 gather_fusion.3
  255.2 2.1 fusion
  257.4 7.1 %scatter_fusion.3 = f32[17,64,128]{2,1,0:T(8,128)S(1)} fusion(f32[17,64,128]{2,1,0:T(8,128)S(1)} %broadcast.70, s32[64]{0:T(128)S(1)} %get-tuple-element.9, f32[64,64,128]{2,1,0:T(8,128)} %fusion), kind=kCustom, calls=%fused_computation.7 | custom fusion | flops 524288 | bytes 6291712 | tf_op jit(solution)/shard_map/scatter-add | solution.py:59
  264.4 0.8 copy_bitcast_fusion
  265.3 1.9 all_gather.10
  267.2 75.5 %reduce-scatter.8.cloned.1.call-done = f32[64,128]{1,0:T(8,128)} async-done(((f32[64,2048]{1,0:T(8,128)}), f32[64,128]{1,0:T(8,128)}) %reduce-scatter.8.cloned.1.call-update) | async-done | bytes 32784 | tf_op jit(solution)/shard_map/reduce_scatter | solution.py:77
  (39 shorter events, 6.1 us)
Async XLA Ops:
  7.2 4.0 %copy-start = (bf16[1,64,128,128]{3,2,1,0:T(8,128)(2,1)S(1)}, bf16[1,64,128,128]{3,2,1,0:T(8,128)(2,1)}, u32[]{:S(2)}) copy-start(bf16[1,64,128,128]{3,2,1,0:T(8,128)(2,1)} %param.12) | copy-start | bytes 6291460
  7.2 4.0 %copy-start.1 = (s32[1,64]{1,0:T(1,128)S(1)}, s32[1,64]{1,0:T(1,128)}, u32[]{:S(2)}) copy-start(s32[1,64]{1,0:T(1,128)} %param.14) | copy-start | bytes 772
  7.2 4.0 %copy-start.2 = (s32[1,64]{1,0:T(1,128)S(1)}, s32[1,64]{1,0:T(1,128)}, u32[]{:S(2)}) copy-start(s32[1,64]{1,0:T(1,128)} %param.13) | copy-start | bytes 772
  7.2 25.3 %reduce-scatter.4.cloned.1.call-start = ((), (), s32[]{:S(2)}) async-start(), calls=%async_computation.3 | async-start | bytes 393216 | tf_op jit(solution)/shard_map/reduce_scatter | solution.py:44
  21.9 175.2 %reduce-scatter.6.cloned.1.call-start = ((), (), s32[]{:S(2)}) async-start(), calls=%async_computation.4 | async-start | bytes 393216 | tf_op jit(solution)/shard_map/reduce_scatter | solution.py:44
  192.9 149.8 %reduce-scatter.8.cloned.1.call-start = ((), (), s32[]{:S(2)}) async-start(), calls=%async_computation.5 | async-start | bytes 557056 | tf_op jit(solution)/shard_map/reduce_scatter | solution.py:77
Sparse Core Ops, SparseCore 0:
  22.0 10.4 reduce-scatter.3
  193.0 4.0 reduce-scatter.5
  265.4 77.2 reduce-scatter.7
where the time goes:
time: 351 us; the launch traced here: 350 us
  blocking collectives  169 us (48%)
  waiting for transfers between devices  90.3 us (26%)
  other arithmetic  53.9 us (15%)
  matrix products  14.9 us (4%)
  between operations  14.7 us (4%)
  local copies, waits for them, and re-layouts  7.35 us (2%)
    psum x1, blocking collectives, local(): next_basis = lax.psum(partial_value, 'cell').astype(jnp.bfloat16)  81.7 us
    psum x2, blocking collectives, first_total(): return lax.psum(gram, ('cell', 'gene'))  81.3 us
    reduce_scatter x1, waiting for transfers between devices, local(): lax.psum_scatter(loadings_of(final_rows), 'cell', scatter_dimension=1, ti...  75.5 us
    reduce_scatter x2, waiting for transfers between devices, merge_halves(): lax.psum_scatter(partial_scores, 'gene', scatter_dimension=1, tiled=True)  14.7 us
    scatter-add x2, other arithmetic, scores_of(): jax.ops.segment_sum(products, row_target, num_segments=row_blocks + 1)  14.1 us
    scatter-add x2, other arithmetic, loadings_of(): jax.ops.segment_sum(products, col_target, num_segments=gene_blocks + 1)  14.1 us
    another operation x6, other arithmetic, orthonormal(): lower_one = jnp.linalg.cholesky(first)  13 us
    another operation x4, other arithmetic, solve_lower(): return lax.linalg.triangular_solve(lower, right, left_side=True, lower=True)  11.1 us
  transfers between devices with their start and end apart: 3, of which 3 were waited for; matrix products, arithmetic and copies ran while one was open for 0% of the time, Pallas kernels for 0%

commit v1 on v0

--- a/solution.py
+++ b/solution.py
@@ -38,7 +38,7 @@
     col_target = jnp.where(live, col_index, gene_blocks)
 
     def first_total(gram):
-        return lax.psum(gram, ("cell", "gene"))
+        return lax.psum(lax.psum(gram, "cell"), "gene")
 
     def merge_halves(partial_scores):
         return lax.psum_scatter(partial_scores, "gene", scatter_dimension=1, tiled=True)

time: 351 us -> 425 us (1.21)
  blocking collectives: 169 us -> 244 us
    psum x2 -> x4, blocking collectives: 81.3 us -> 161 us  [first_total(): return lax.psum(lax.psum(gram, 'cell'), 'gene')]
    psum x1, blocking collectives: 81.7 us -> 77.3 us  [local(): next_basis = lax.psum(partial_value, 'cell').astype(jnp.bfloat16)]
where the time goes in v1:
time: 425 us; the launch traced here: 423 us
  blocking collectives  244 us (57%)
  waiting for transfers between devices  88.7 us (21%)
  other arithmetic  53.9 us (13%)
  matrix products  14.9 us (4%)
  between operations  14.7 us (3%)
  local copies, waits for them, and re-layouts  7.35 us (2%)
    psum x4, blocking collectives, first_total(): return lax.psum(lax.psum(gram, 'cell'), 'gene')  161 us
    psum x1, blocking collectives, local(): next_basis = lax.psum(partial_value, 'cell').astype(jnp.bfloat16)  77.3 us
    reduce_scatter x1, waiting for transfers between devices, local(): lax.psum_scatter(loadings_of(final_rows), 'cell', scatter_dimension=1, ti...  72 us
    reduce_scatter x2, waiting for transfers between devices, merge_halves(): lax.psum_scatter(partial_scores, 'gene', scatter_dimension=1, tiled=True)  16.6 us
    scatter-add x2, other arithmetic, scores_of(): jax.ops.segment_sum(products, row_target, num_segments=row_blocks + 1)  14.1 us
    scatter-add x2, other arithmetic, loadings_of(): jax.ops.segment_sum(products, col_target, num_segments=gene_blocks + 1)  14.1 us
    another operation x6, other arithmetic, orthonormal(): lower_one = jnp.linalg.cholesky(first)  13 us
    another operation x4, other arithmetic, solve_lower(): return lax.linalg.triangular_solve(lower, right, left_side=True, lower=True)  11.1 us
  transfers between devices with their start and end apart: 3, of which 3 were waited for; matrix products, arithmetic and copies ran while one was open for 0% of the time, Pallas kernels for 0%

profile of v1, /device:TPU:0, one launch (start us, length us, event | category | flops | bytes accessed | tf_op | source)
XLA Modules:
  0.0 423.5 jit_solution(6048577465296254689)
XLA Ops:
  7.2 0.8 compare_select_fusion
  8.7 1.0 copy_bitcast_fusion.5
  10.4 0.7 gather_fusion
  11.2 2.9 fusion.6
  14.1 7.1 %scatter_fusion = f32[9,64,128]{2,1,0:T(8,128)S(1)} fusion(f32[9,64,128]{2,1,0:T(8,128)S(1)} %broadcast.69.clone, s32[64]{0:T(128)S(1)} %get-tuple-element.8, f32[64,64,128]{2,1,0:T(8,128)} %fusion.6), kind=kCustom, calls=%fused_computation.4 | custom fusion | flops 524288 | bytes 6291712 | tf_op jit(solution)/shard_map/scatter-add | solution.py:51
  22.0 10.5 %reduce-scatter.4.cloned.1.call-done = f32[64,512]{1,0:T(8,128)} async-done(((f32[64,1024]{1,0:T(8,128)}), f32[64,512]{1,0:T(8,128)}) %reduce-scatter.4.cloned.1.call-update) | async-done | bytes 131088 | tf_op jit(solution)/shard_map/reduce_scatter | solution.py:44
  32.5 1.2 fusion.40
  33.8 77.0 %psum.35 = f32[64,64]{0,1:T(8,128)S(1)} all-reduce(f32[64,64]{0,1:T(8,128)S(1)} %fusion.40), channel_id=1, replica_groups=mesh['cell'=16,'gene'=2] {'cell'}, use_global_device_ids=true, to_apply=%region_2.4 | all-reduce | flops 4096 | bytes 32768 | tf_op jit(solution)/shard_map/psum | solution.py:41
  110.7 3.4 psum.36
  114.2 5.8 %cholesky.44 = f32[64,64]{1,0:T(8,128)S(1)} custom-call(f32[64,64]{1,0:T(8,128)S(1)} %fusion.30), custom_call_target="Cholesky" | custom-call | tf_op jit(solution)/shard_map/jit(cholesky)/cholesky | solution.py:21
  121.4 4.9 %custom-call.6 = f32[1,64,64]{1,2,0:T(8,128)S(1)} custom-call(f32[1,64,64]{2,1,0:T(8,128)S(1)} %fusion.24), custom_call_target="InvertDiagBlocksLowerTriangular" | custom-call | tf_op jit(solution)/shard_map/triangular_solve/custom-call.0 | solution.py:10
  126.3 1.2 convolution_convert_fusion
  127.6 1.9 all_gather.9
  130.2 2.1 fusion.4
  132.4 7.1 %scatter_fusion.1 = f32[17,64,128]{2,1,0:T(8,128)S(1)} fusion(f32[17,64,128]{2,1,0:T(8,128)S(1)} %broadcast.70.clone, s32[64]{0:T(128)S(1)} %get-tuple-element.9, f32[64,64,128]{2,1,0:T(8,128)} %fusion.4), kind=kCustom, calls=%fused_computation.5 | custom fusion | flops 524288 | bytes 6291712 | tf_op jit(solution)/shard_map/scatter-add | solution.py:59
  139.5 77.3 %all-reduce.1 = bf16[64,2048]{1,0:T(8,128)(2,1)S(1)} all-reduce(f32[64,2048]{1,0:T(8,128)S(1)} %copy_bitcast_fusion.1), channel_id=1, replica_groups=mesh['cell'=16,'gene'=2] {'cell'}, use_global_device_ids=true, to_apply=%region_7.12 | all-reduce | flops 131072 | bytes 786432 | tf_op jit(solution)/shard_map/psum | solution.py:68
  216.9 0.8 gather_fusion.2
  217.6 2.9 fusion.2
  220.6 7.1 %scatter_fusion.2 = f32[9,64,128]{2,1,0:T(8,128)S(1)} fusion(f32[9,64,128]{2,1,0:T(8,128)S(1)} %broadcast.69, s32[64]{0:T(128)S(1)} %get-tuple-element.8, f32[64,64,128]{2,1,0:T(8,128)} %fusion.2), kind=kCustom, calls=%fused_computation.6 | custom fusion | flops 524288 | bytes 6291712 | tf_op jit(solution)/shard_map/scatter-add | solution.py:51
  228.4 6.1 %reduce-scatter.6.cloned.1.call-done = f32[64,512]{1,0:T(8,128)} async-done(((f32[64,1024]{1,0:T(8,128)}), f32[64,512]{1,0:T(8,128)}) %reduce-scatter.6.cloned.1.call-update) | async-done | bytes 131088 | tf_op jit(solution)/shard_map/reduce_scatter | solution.py:44
  234.5 1.2 fusion.41
  235.8 77.0 %psum.38 = f32[64,64]{0,1:T(8,128)S(1)} all-reduce(f32[64,64]{0,1:T(8,128)S(1)} %fusion.41), channel_id=1, replica_groups=mesh['cell'=16,'gene'=2] {'cell'}, use_global_device_ids=true, to_apply=%region_10.15 | all-reduce | flops 4096 | bytes 32768 | tf_op jit(solution)/shard_map/psum | solution.py:41
  312.8 3.4 psum.39
  316.3 5.8 %cholesky.55 = f32[64,64]{1,0:T(8,128)S(1)} custom-call(f32[64,64]{1,0:T(8,128)S(1)} %fusion.28), custom_call_target="Cholesky" | custom-call | tf_op jit(solution)/shard_map/jit(cholesky)/cholesky | solution.py:21
  323.4 4.9 %custom-call.7 = f32[1,64,64]{1,2,0:T(8,128)S(1)} custom-call(f32[1,64,64]{2,1,0:T(8,128)S(1)} %fusion.25), custom_call_target="InvertDiagBlocksLowerTriangular" | custom-call | tf_op jit(solution)/shard_map/triangular_solve/custom-call.0 | solution.py:10
  328.3 1.2 fusion.39
  329.6 1.9 all_gather.11
  332.3 2.1 fusion
  334.4 7.1 %scatter_fusion.3 = f32[17,64,128]{2,1,0:T(8,128)S(1)} fusion(f32[17,64,128]{2,1,0:T(8,128)S(1)} %broadcast.70, s32[64]{0:T(128)S(1)} %get-tuple-element.9, f32[64,64,128]{2,1,0:T(8,128)} %fusion), kind=kCustom, calls=%fused_computation.7 | custom fusion | flops 524288 | bytes 6291712 | tf_op jit(solution)/shard_map/scatter-add | solution.py:59
  341.5 0.8 copy_bitcast_fusion
  342.3 1.9 all_gather.10
  344.2 72.0 %reduce-scatter.8.cloned.1.call-done = f32[64,128]{1,0:T(8,128)} async-done(((f32[64,2048]{1,0:T(8,128)}), f32[64,128]{1,0:T(8,128)}) %reduce-scatter.8.cloned.1.call-update) | async-done | bytes 32784 | tf_op jit(solution)/shard_map/reduce_scatter | solution.py:77
  (41 shorter events, 7.6 us)
Async XLA Ops:
  7.2 4.0 copy-start
  7.2 4.0 copy-start.1
  7.2 4.0 copy-start.2
  7.2 25.3 %reduce-scatter.4.cloned.1.call-start = ((), (), s32[]{:S(2)}) async-start(), calls=%async_computation.3 | async-start | bytes 393216 | tf_op jit(solution)/shard_map/reduce_scatter | solution.py:44
  21.9 212.6 %reduce-scatter.6.cloned.1.call-start = ((), (), s32[]{:S(2)}) async-start(), calls=%async_computation.4 | async-start | bytes 393216 | tf_op jit(solution)/shard_map/reduce_scatter | solution.py:44
  228.4 187.9 %reduce-scatter.8.cloned.1.call-start = ((), (), s32[]{:S(2)}) async-start(), calls=%async_computation.5 | async-start | bytes 557056 | tf_op jit(solution)/shard_map/reduce_scatter | solution.py:77
Sparse Core Ops, SparseCore 0:
  22.0 10.4 reduce-scatter.3
  228.5 5.9 reduce-scatter.5
  342.4 73.7 reduce-scatter.7
